TPU v7x, 256 devices: a whole 4x4x8 slice. The times are simulated.
256 devices in a mesh: seq: 64 (over z, y, core), head: 4 (over x).
Axes of the slice: x: 4, y: 4, z: 8, core: 2. Of those that a mesh axis runs over, the one named last changes fastest.
Arguments:
- queries: bfloat16 [16384, 4096], P('seq', 'head'), may hold values from -5 to 5
- keys: bfloat16 [16384, 4096], P('seq', 'head'), may hold values from -5 to 5
- values: bfloat16 [16384, 4096], P('seq', 'head'), may hold values from -6 to 6
- beta: float32 [32], P('head'), may hold values from -2 to 2
- w_out: bfloat16 [4096, 4096], P('head'), may hold values from -0.09375 to 0.09375
Outputs:
- mixed: bfloat16 [16384, 4096], P('seq', 'head')
All inputs are finite; a program needn't handle non-finite values.
Results may differ from a plain program's by a relative error of at most 0.0069.
Values may be sent and summed in bfloat16 or wider, within the bound.
A program may use at most 192 MiB of HBM per device.

v0:
```python
import jax
import jax.numpy as jnp
from jax import lax
from jax.sharding import Mesh
from jax.sharding import PartitionSpec as P

HD = 128
SEG = 2048
SEQ = ("seq_0", "seq_1", "seq_2")


def passed_along(block, axis, distance):
    devices = range(lax.axis_size(axis))
    route = [(i - distance, i) for i in devices if i - distance in devices]
    return lax.ppermute(block, axis, route)


def filled_with(value, identity):
    return jax.tree.map(
        lambda a, e: jnp.broadcast_to(jnp.asarray(e, a.dtype), a.shape), value, identity
    )


def prefix_by_axis(value, axes, combine, identity):
    before = start = filled_with(value, identity)
    total = value
    for axis in reversed(axes):
        length, position = (lax.axis_size(axis), lax.axis_index(axis))
        pieces = jax.tree.map(lambda part: lax.all_gather(part, axis), total)
        inside, total = (start, start)
        for k in range(length):
            passed = k < position
            total = combine(total, jax.tree.map(lambda part: part[k], pieces))
            inside = jax.tree.map(lambda new, old: jnp.where(passed, new, old), total, inside)
        before = combine(inside, before)
    return before


def cut_along(value, dim, length):
    lengths = value.shape
    pieces = value.reshape(*lengths[:dim], length, lengths[dim] // length, *lengths[dim + 1 :])
    return jnp.moveaxis(pieces, dim, 0)


def summed_on_arrival(value, axis, dim):
    length = lax.axis_size(axis)
    pieces = lax.all_to_all(cut_along(value, dim, length), axis, 0, 0, tiled=True)
    return jnp.sum(pieces.astype(jnp.float32), axis=0)


def elu_plus(inputs):
    return jnp.where(inputs > 0, inputs + 1.0, jnp.exp(jnp.minimum(inputs, 0.0)))


def add_pair(earlier, later):
    return (earlier[0] + later[0], earlier[1] + later[1])


def memory_terms(key_block, value_block, heads_here, row_weight):
    token_rows = key_block.shape[0]
    soft_keys = elu_plus(key_block.astype(jnp.float32)).astype(jnp.bfloat16)
    soft_keys = (soft_keys * row_weight[:, None]).reshape(token_rows, heads_here, HD)
    shaped_values = value_block.reshape(token_rows, heads_here, HD)
    outer = jnp.einsum("thd,the->hde", soft_keys, shaped_values, preferred_element_type=jnp.float32)
    totals = jnp.sum(soft_keys, axis=0, dtype=jnp.float32)
    return (outer, totals)


def body(queries, keys, values, beta, w_out):
    token_rows, width = queries.shape
    heads_here = width // HD
    groups = SEG // token_rows
    seq_rank = lax.axis_index(SEQ)
    place = seq_rank % groups
    stacked = jnp.stack((keys, values))
    earlier_blocks = []
    moving = stacked
    for distance in range(1, groups + 1):
        moving = passed_along(moving, SEQ, 1)
        earlier_blocks.append(moving)
    ordered = earlier_blocks[::-1] + [stacked]
    all_keys = jnp.concatenate([block[0] for block in ordered], axis=0)
    all_values = jnp.concatenate([block[1] for block in ordered], axis=0)
    own_ones = jnp.ones((token_rows,), jnp.bfloat16)
    own_outer, own_totals = memory_terms(keys, values, heads_here, own_ones)
    zero_mem = jnp.zeros((heads_here, HD, HD), jnp.float32)
    zero_norm = jnp.zeros((heads_here, HD), jnp.float32)
    memory, norm_prev = prefix_by_axis(
        (own_outer, own_totals), SEQ, add_pair, (zero_mem, zero_norm)
    )
    earlier_rows = groups * token_rows
    row_distance = groups - jnp.arange(earlier_rows) // token_rows
    inside = ((row_distance <= place) & (row_distance < groups)).astype(jnp.bfloat16)
    outer, totals = memory_terms(
        all_keys[:earlier_rows], all_values[:earlier_rows], heads_here, inside
    )
    memory = memory - outer
    norm_prev = norm_prev - totals
    soft_queries = lax.optimization_barrier(
        elu_plus(queries.astype(jnp.float32)).astype(jnp.bfloat16)
    )
    soft_queries = soft_queries.astype(jnp.float32).reshape(token_rows, heads_here, HD)
    numer = jnp.einsum("thd,hde->the", soft_queries, memory, precision=lax.Precision.HIGHEST)
    denom = 1.0 + jnp.einsum("thd,hd->th", soft_queries, norm_prev, precision=lax.Precision.HIGHEST)
    from_memory = numer / denom[..., None]
    scale = HD ** (-0.5)
    key_offset = jnp.arange((groups + 1) * token_rows) - groups * token_rows
    query_offset = jnp.arange(token_rows)
    visible = (
        (key_offset[None, :] <= query_offset[:, None])
        & (key_offset[None, :] > query_offset[:, None] - SEG)
        & (seq_rank * token_rows + key_offset[None, :] >= 0)
    )
    gates = jax.nn.sigmoid(beta)
    outputs = []
    for head_index in range(heads_here):
        lower = head_index * HD
        query_head = queries[:, lower : lower + HD]
        key_head = all_keys[:, lower : lower + HD]
        value_head = all_values[:, lower : lower + HD]
        scores = (
            lax.dot_general(
                query_head, key_head, (((1,), (1,)), ((), ())), preferred_element_type=jnp.float32
            )
            * scale
        )
        scores = jnp.where(visible, scores, -jnp.inf)
        highest = jnp.max(scores, axis=1, keepdims=True)
        weights = jnp.exp(scores - highest)
        total = jnp.sum(weights, axis=1, keepdims=True)
        local = (
            jnp.dot(weights.astype(jnp.bfloat16), value_head, preferred_element_type=jnp.float32)
            / total
        )
        gate = gates[head_index]
        outputs.append(
            (gate * from_memory[:, head_index] + (1.0 - gate) * local).astype(jnp.bfloat16)
        )
    attended = jnp.concatenate(outputs, axis=1)
    partial_out = jnp.dot(attended, w_out, preferred_element_type=jnp.float32)
    summed = summed_on_arrival(partial_out.astype(jnp.bfloat16), "head", 1)
    return summed.astype(jnp.bfloat16)


def solution(mesh):
    torus = Mesh(
        mesh.devices.reshape(8, 4, 2, mesh.shape["head"]), ("seq_0", "seq_1", "seq_2", "head")
    )
    return jax.shard_map(
        body,
        mesh=torus,
        in_specs=(P(SEQ, "head"), P(SEQ, "head"), P(SEQ, "head"), P("head"), P("head", None)),
        out_specs=P(SEQ, "head"),
        check_vma=False,
    )
```

profile of v0, /device:TPU:160, one launch (start us, length us, event | category | flops | bytes accessed | tf_op | source)
XLA Modules:
  0.0 316.4 jit_solution(12599963364403843043)
XLA Ops:
  9.8 16.3 %collective-permute-done = bf16[2,256,1024]{2,1,0:T(8,128)(2,1)S(1)} collective-permute-done((bf16[2,256,1024]{2,1,0:T(8,128)(2,1)S(1)}, bf16[2,256,1024]{2,1,0:T(8,128)(2,1)S(1)}, u32[]{:S(2)}, u32[]{:S(2)}) %collective-permute-start) | collective-permute-done | bytes 1048608 | tf_op jit(solution)/shard_map/ppermute | solution.py:15
  28.0 16.3 %collective-permute-done.1 = bf16[2,256,1024]{2,1,0:T(8,128)(2,1)S(1)} collective-permute-done((bf16[2,256,1024]{2,1,0:T(8,128)(2,1)S(1)}, bf16[2,256,1024]{2,1,0:T(8,128)(2,1)S(1)}, u32[]{:S(2)}, u32[]{:S(2)}) %collective-permute-start.1) | collective-permute-done | bytes 1048608 | tf_op jit(solution)/shard_map/ppermute | solution.py:15
  49.6 13.0 %collective-permute-done.2 = bf16[2,256,1024]{2,1,0:T(8,128)(2,1)} collective-permute-done((bf16[2,256,1024]{2,1,0:T(8,128)(2,1)S(1)}, bf16[2,256,1024]{2,1,0:T(8,128)(2,1)}, u32[]{:S(2)}, u32[]{:S(2)}) %collective-permute-start.2) | collective-permute-done | bytes 1048608 | tf_op jit(solution)/shard_map/ppermute | solution.py:15
  65.8 15.4 %collective-permute-done.3 = bf16[2,256,1024]{2,1,0:T(8,128)(2,1)} collective-permute-done((bf16[2,256,1024]{2,1,0:T(8,128)(2,1)}, bf16[2,256,1024]{2,1,0:T(8,128)(2,1)}, u32[]{:S(2)}, u32[]{:S(2)}) %collective-permute-start.3) | collective-permute-done | bytes 1048608 | tf_op jit(solution)/shard_map/ppermute | solution.py:15
  89.2 10.5 %collective-permute-done.4 = bf16[2,256,1024]{2,1,0:T(8,128)(2,1)} collective-permute-done((bf16[2,256,1024]{2,1,0:T(8,128)(2,1)}, bf16[2,256,1024]{2,1,0:T(8,128)(2,1)}, u32[]{:S(2)}, u32[]{:S(2)}) %collective-permute-start.4) | collective-permute-done | bytes 1048608 | tf_op jit(solution)/shard_map/ppermute | solution.py:15
  101.7 18.1 %all_gather.34 = f32[4,8,128]{2,1,0:T(8,128)S(1)} all-gather(f32[1,8,128]{2,1,0:T(8,128)S(1)} %slice_add_fusion.21), channel_id=1, replica_groups=mesh['seq_0'=8,'seq_1'=4,'seq_2'=2,'head'=4] {'seq_1'}, dimensions={0}, use_global_device_ids=true | all-gather | bytes 20480 | tf_op jit(solution)/shard_map/all_gather | solution.py:29
  130.7 29.8 %all_gather.35 = f32[8,8,128]{2,1,0:T(8,128)S(1)} all-gather(f32[1,8,128]{2,1,0:T(8,128)S(1)} %slice_add_fusion.18), channel_id=1, replica_groups=mesh['seq_0'=8,'seq_1'=4,'seq_2'=2,'head'=4] {'seq_0'}, dimensions={0}, use_global_device_ids=true | all-gather | bytes 36864 | tf_op jit(solution)/shard_map/all_gather | solution.py:29
  172.3 2.4 fusion.223
  179.2 6.7 %collective-permute-done.7 = bf16[2,256,1024]{2,1,0:T(8,128)(2,1)} collective-permute-done((bf16[2,256,1024]{2,1,0:T(8,128)(2,1)}, bf16[2,256,1024]{2,1,0:T(8,128)(2,1)}, u32[]{:S(2)}, u32[]{:S(2)}) %collective-permute-start.7) | collective-permute-done | bytes 1048608 | tf_op jit(solution)/shard_map/ppermute | solution.py:15
  201.9 3.2 %fusion.255 = (f32[256]{0:T(256)S(1)}, f32[256,2304]{0,1:T(8,128)S(1)}) fusion(bf16[256,1024]{1,0:T(8,128)(2,1)} %param.5, bf16[2304,1024]{1,0:T(8,128)(2,1)} %copy-done.29, pred[2304]{0:T(1024)(128)(4,1)S(1)} %add_compare_fusion, s32[256]{0:T(256)S(1)} %iota_add_fusion.1, s32[2304]{0:T(1024)S(1)} %iota_add_fusion), kind=kOutput, calls=%fused_computation.296 | convolution fusion | flops 155123456 | bytes 3028224 | tf_op jit(solution)/shard_map/dot_general | solution.py:122
  206.8 3.0 fusion.256
  211.6 3.0 fusion.257
  216.4 3.0 fusion.258
  221.3 3.0 fusion.259
  226.1 3.0 fusion.260
  231.0 3.0 fusion.261
  234.4 3.3 %fusion.262 = (f32[256]{0:T(256)S(1)}, f32[256,2304]{0,1:T(8,128)S(1)}) fusion(bf16[256,1024]{1,0:T(8,128)(2,1)} %param.5, bf16[2304,1024]{1,0:T(8,128)(2,1)} %copy-done.29, pred[2304]{0:T(1024)(128)(4,1)S(1)} %add_compare_fusion, s32[256]{0:T(256)S(1)} %iota_add_fusion.1, s32[2304]{0:T(1024)S(1)} %iota_add_fusion), kind=kOutput, calls=%fused_computation.303 | convolution fusion | flops 155123456 | bytes 3028224 | tf_op jit(solution)/shard_map/dot_general | solution.py:122
  238.1 2.5 convert_reduce_fusion
  241.0 7.9 %fusion.7 = bf16[2048,8,128]{2,1,0:T(8,128)(2,1)} fusion(bf16[2048,8,128]{2,1,0:T(8,128)(2,1)S(1)} %constant_dynamic-update-slice_fusion, bf16[2048]{0:T(1024)(128)(2,1)S(1)} %fusion.247), kind=kLoop, calls=%fused_computation.23 | loop fusion | flops 14680064 | bytes 8392704 | tf_op jit(solution)/shard_map/mul | solution.py:62
  248.9 8.4 %fusion.46 = f32[8,128,128]{2,1,0:T(8,128)S(1)} fusion(bf16[2048,8,128]{2,1,0:T(8,128)(2,1)} %copy-done.28, bf16[2048,8,128]{2,1,0:T(8,128)(2,1)} %fusion.7, f32[8,8,128,128]{3,2,1,0:T(8,128)} %all-gather.6.cloned.1.call-done, f32[1,8,128,128]{3,2,1,0:T(8,128)S(1)} %copy-done.17, f32[8,128,128]{2,1,0:T(8,128)S(1)} %copy-done.16, ...), kind=kOutput, calls=%fused_computation.79 | convolution fusion | flops 540278784 | bytes 16252942 | tf_op jit(solution)/shard_map/thd,the->hde/dot_general | solution.py:64
  258.0 2.9 fusion.192
  265.7 2.6 fusion.174
  270.6 2.4 fusion.162
  280.0 28.6 %all_to_all.5 = bf16[4,256,1024]{2,1,0:T(8,128)(2,1)S(1)} all-to-all(bf16[4,256,1024]{2,1,0:T(8,128)(2,1)S(1)} %bitcast.238), channel_id=1, replica_groups=mesh['seq_0'=8,'seq_1'=4,'seq_2'=2,'head'=4] {'head'}, dimensions={0} | all-to-all | bytes 4194304 | tf_op jit(solution)/shard_map/all_to_all | solution.py:47
  (174 shorter events, 89.1 us)
Async XLA Ops:
  6.5 58.1 %copy-start = (bf16[256,1024]{1,0:T(8,128)(2,1)S(1)}, bf16[256,1024]{1,0:T(8,128)(2,1)}, u32[]{:S(2)}) copy-start(bf16[256,1024]{1,0:T(8,128)(2,1)} %param.7) | copy-start | bytes 1572868
  6.5 78.7 %all-gather.8.cloned.1.call-start = ((), (), s32[]{:S(2)}) async-start(), calls=%async_computation.2 | async-start | bytes 1572864 | tf_op jit(solution)/shard_map/all_gather | solution.py:29
  6.5 113.2 %copy-start.31 = (f32[8]{0:T(128)S(1)}, f32[8]{0:T(128)}, u32[]{:S(2)}) copy-start(f32[8]{0:T(128)} %param.8) | copy-start | bytes 100
  7.9 18.2 %collective-permute-start = (bf16[2,256,1024]{2,1,0:T(8,128)(2,1)S(1)}, bf16[2,256,1024]{2,1,0:T(8,128)(2,1)S(1)}, u32[]{:S(2)}, u32[]{:S(2)}) collective-permute-start(bf16[2,256,1024]{2,1,0:T(8,128)(2,1)S(1)} %pad_maximum_fusion), channel_id=1, source_target_pairs={{0,4},{4,8},{8,12},{12,16},{16,20},{20,24},{24,28},{28,32},{32,36}... | collective-permute-start | bytes 3145736 | tf_op jit(solution)/shard_map/ppermute | solution.py:15
  26.1 18.2 %collective-permute-start.1 = (bf16[2,256,1024]{2,1,0:T(8,128)(2,1)S(1)}, bf16[2,256,1024]{2,1,0:T(8,128)(2,1)S(1)}, u32[]{:S(2)}, u32[]{:S(2)}) collective-permute-start(bf16[2,256,1024]{2,1,0:T(8,128)(2,1)S(1)} %collective-permute-done), channel_id=1, source_target_pairs={{0,4},{4,8},{8,12},{12,16},{16,20},{20,24},{24,28},{28,32},{32,36}... | collective-permute-start | bytes 3145736 | tf_op jit(solution)/shard_map/ppermute | solution.py:15
  44.3 18.3 %collective-permute-start.2 = (bf16[2,256,1024]{2,1,0:T(8,128)(2,1)S(1)}, bf16[2,256,1024]{2,1,0:T(8,128)(2,1)}, u32[]{:S(2)}, u32[]{:S(2)}) collective-permute-start(bf16[2,256,1024]{2,1,0:T(8,128)(2,1)S(1)} %collective-permute-done.1), channel_id=1, source_target_pairs={{0,4},{4,8},{8,12},{12,16},{16,20},{20,24},{24,28},{28,32},{32,36}... | collective-permute-start | bytes 3145736 | tf_op jit(solution)/shard_map/ppermute | solution.py:15
  62.7 18.5 %collective-permute-start.3 = (bf16[2,256,1024]{2,1,0:T(8,128)(2,1)}, bf16[2,256,1024]{2,1,0:T(8,128)(2,1)}, u32[]{:S(2)}, u32[]{:S(2)}) collective-permute-start(bf16[2,256,1024]{2,1,0:T(8,128)(2,1)} %collective-permute-done.2), channel_id=1, source_target_pairs={{0,4},{4,8},{8,12},{12,16},{16,20},{20,24},{24,28},{28,32},{32,36}... | collective-permute-start | bytes 3145736 | tf_op jit(solution)/shard_map/ppermute | solution.py:15
  65.7 106.6 %all-gather.10.cloned.1.call-start = ((), (), s32[]{:S(2)}) async-start(), calls=%async_computation.3 | async-start | bytes 2621440 | tf_op jit(solution)/shard_map/all_gather | solution.py:29
  81.2 18.5 %collective-permute-start.4 = (bf16[2,256,1024]{2,1,0:T(8,128)(2,1)}, bf16[2,256,1024]{2,1,0:T(8,128)(2,1)}, u32[]{:S(2)}, u32[]{:S(2)}) collective-permute-start(bf16[2,256,1024]{2,1,0:T(8,128)(2,1)} %collective-permute-done.3), channel_id=1, source_target_pairs={{0,4},{4,8},{8,12},{12,16},{16,20},{20,24},{24,28},{28,32},{32,36}... | collective-permute-start | bytes 3145736 | tf_op jit(solution)/shard_map/ppermute | solution.py:15
  87.4 161.5 %all-gather.6.cloned.1.call-start = ((), (), s32[]{:S(2)}) async-start(), calls=%async_computation.1 | async-start | bytes 4718592 | tf_op jit(solution)/shard_map/all_gather | solution.py:29
  99.7 22.8 %collective-permute-start.5 = (bf16[2,256,1024]{2,1,0:T(8,128)(2,1)}, bf16[2,256,1024]{2,1,0:T(8,128)(2,1)}, u32[]{:S(2)}, u32[]{:S(2)}) collective-permute-start(bf16[2,256,1024]{2,1,0:T(8,128)(2,1)} %collective-permute-done.4), channel_id=1, source_target_pairs={{0,4},{4,8},{8,12},{12,16},{16,20},{20,24},{24,28},{28,32},{32,36}... | collective-permute-start | bytes 3145736 | tf_op jit(solution)/shard_map/ppermute | solution.py:15
  122.5 44.8 %collective-permute-start.6 = (bf16[2,256,1024]{2,1,0:T(8,128)(2,1)}, bf16[2,256,1024]{2,1,0:T(8,128)(2,1)}, u32[]{:S(2)}, u32[]{:S(2)}) collective-permute-start(bf16[2,256,1024]{2,1,0:T(8,128)(2,1)} %collective-permute-done.5), channel_id=1, source_target_pairs={{0,4},{4,8},{8,12},{12,16},{16,20},{20,24},{24,28},{28,32},{32,36}... | collective-permute-start | bytes 3145736 | tf_op jit(solution)/shard_map/ppermute | solution.py:15
  125.8 114.9 %copy-start.18 = (bf16[256,1024]{0,1:T(8,128)(2,1)}, bf16[256,1024]{0,1:T(8,128)(2,1)S(1)}, u32[]{:S(2)}) copy-start(bf16[256,1024]{0,1:T(8,128)(2,1)S(1)} %copy.22) | copy-start | bytes 1572868
  167.4 18.5 %collective-permute-start.7 = (bf16[2,256,1024]{2,1,0:T(8,128)(2,1)}, bf16[2,256,1024]{2,1,0:T(8,128)(2,1)}, u32[]{:S(2)}, u32[]{:S(2)}) collective-permute-start(bf16[2,256,1024]{2,1,0:T(8,128)(2,1)} %collective-permute-done.6), channel_id=1, source_target_pairs={{0,4},{4,8},{8,12},{12,16},{16,20},{20,24},{24,28},{28,32},{32,36}... | collective-permute-start | bytes 3145736 | tf_op jit(solution)/shard_map/ppermute | solution.py:15
  241.0 7.9 %copy-start.16 = (f32[8,128,128]{2,1,0:T(8,128)S(1)}, f32[8,128,128]{2,1,0:T(8,128)}, u32[]{:S(2)}) copy-start(f32[8,128,128]{2,1,0:T(8,128)} %slice_add_fusion.10) | copy-start | bytes 1572868
  241.0 7.9 %copy-start.17 = (f32[1,8,128,128]{3,2,1,0:T(8,128)S(1)}, f32[1,8,128,128]{3,2,1,0:T(8,128)}, u32[]{:S(2)}) copy-start(f32[1,8,128,128]{3,2,1,0:T(8,128)} %fusion.223) | copy-start | bytes 1572868
  248.9 8.4 %copy-start.19 = (bf16[256,1024]{0,1:T(8,128)(2,1)S(1)}, bf16[256,1024]{0,1:T(8,128)(2,1)}, u32[]{:S(2)}) copy-start(bf16[256,1024]{0,1:T(8,128)(2,1)} %copy-done.18) | copy-start | bytes 1572868
  248.9 9.0 %copy-start.15 = (f32[256,2304]{0,1:T(8,128)S(1)}, f32[256,2304]{0,1:T(8,128)}, u32[]{:S(2)}) copy-start(f32[256,2304]{0,1:T(8,128)} %copy-done.14) | copy-start | bytes 7077892
  257.9 7.7 %copy-start.9 = (f32[256,2304]{0,1:T(8,128)S(1)}, f32[256,2304]{0,1:T(8,128)}, u32[]{:S(2)}) copy-start(f32[256,2304]{0,1:T(8,128)} %copy-done.8) | copy-start | bytes 7077892
  260.8 7.5 %copy-start.7 = (f32[256,2304]{0,1:T(8,128)S(1)}, f32[256,2304]{0,1:T(8,128)}, u32[]{:S(2)}) copy-start(f32[256,2304]{0,1:T(8,128)} %copy-done.6) | copy-start | bytes 7077892
  263.2 7.3 %copy-start.5 = (f32[256,2304]{0,1:T(8,128)S(1)}, f32[256,2304]{0,1:T(8,128)}, u32[]{:S(2)}) copy-start(f32[256,2304]{0,1:T(8,128)} %copy-done.4) | copy-start | bytes 7077892
  265.7 7.4 %copy-start.3 = (f32[256,2304]{0,1:T(8,128)S(1)}, f32[256,2304]{0,1:T(8,128)}, u32[]{:S(2)}) copy-start(f32[256,2304]{0,1:T(8,128)} %copy-done.2) | copy-start | bytes 7077892
  265.7 11.7 %slice-start = ((s8[8388608]{0:T(1024)(128)(4,1)}), s8[4194304]{0:T(1024)(128)(4,1)S(1)}, s32[]{:S(2)}) async-start(s8[8388608]{0:T(1024)(128)(4,1)} %bitcast.235), calls=%async_computation.4 | async-start | bytes 8388608
  270.6 6.8 %slice-start.1 = ((s8[8388608]{0:T(1024)(128)(4,1)}), s8[4194304]{0:T(1024)(128)(4,1)S(1)}, s32[]{:S(2)}) async-start(s8[8388608]{0:T(1024)(128)(4,1)} %bitcast.235), calls=%async_computation.5 | async-start | bytes 8388608
  (21 other events, 47.6 us)
Sparse Core Ops, SparseCore 0:
  65.8 19.4 all-gather.7
  87.5 59.2 all-gather.9
  174.9 57.7 all-gather.5
where the time goes:
time: 322 us; the launch traced here: 316 us
  waiting for transfers between devices  80.5 us (25%)
  blocking collectives  78.3 us (24%)
  matrix products  56.6 us (18%)
  local copies, waits for them, and re-layouts  41.8 us (13%)
  other arithmetic  25 us (8%)
  between operations  19 us (6%)
  starting transfers between devices  15.4 us (5%)
    ppermute x8, waiting for transfers between devices, passed_along(): return lax.ppermute(block, axis, route)  78.2 us
    all_gather x3, blocking collectives, prefix_by_axis(): pieces = jax.tree.map(lambda part: lax.all_gather(part, axis), total)  49.7 us
    unnamed x113, local copies, waits for them, and re-layouts  38 us
    all_to_all x1, blocking collectives, summed_on_arrival(): lax.all_to_all(cut_along(value, dim, length), axis, 0, 0, tiled=True)  28.6 us
    dot_general x8, matrix products, body(): lax.dot_general(query_head, key_head, (((1,), (1,)), ((), ())), preferred...  24.5 us
    dot_general x8, matrix products, body(): jnp.dot(weights.astype(jnp.bfloat16), value_head, preferred_element_type=...  19.3 us
    ppermute x8, starting transfers between devices, passed_along(): return lax.ppermute(block, axis, route)  15.3 us
    dot_general x2, matrix products, memory_terms(): jnp.einsum('thd,the->hde', soft_keys, shaped_values, preferred_element_ty...  9.44 us
  transfers between devices with their start and end apart: 11, of which 7 were waited for; matrix products, arithmetic and copies ran while one was open for 25% of the time, Pallas kernels for 0%

commit v1 on v0

v1 whole, which is shorter than its diff:
```python
import functools

import jax
import jax.numpy as jnp
from jax import lax
from jax.experimental import pallas as pl
from jax.experimental.pallas import tpu as pltpu
from jax.sharding import Mesh
from jax.sharding import PartitionSpec as P

HD = 128
ROWS = 256
NB = 8
SEG = NB * ROWS
SEQ = ("seq_0", "seq_1", "seq_2")
MESH = pl.DeviceIdType.MESH
BF = jnp.bfloat16
F32 = jnp.float32
SCALE2 = (HD ** -0.5) * 1.4426950408889634
FIRST = 5


def rows(block):
    return pl.ds(pl.multiple_of(block * ROWS, ROWS), ROWS)


def cols(head):
    return pl.ds(pl.multiple_of(head * HD, HD), HD)


def group_id(block):
    return {"seq_1": block // 2, "seq_2": block % 2}


def phi(x):
    return jnp.where(x > 0, x + 1.0, jnp.exp(jnp.minimum(x, 0.0)))


def body(q_hbm, k_hbm, v_hbm, beta_ref, w_hbm, out_ref,
         kcat, vcat, qh, wv, terms, tmsg, tin, mem, att_out, att_in,
         relay_out, relay_in, part_out, part_in,
         ss, rs, zs, zr, ts, tr, as_, ar, xs, xr, wsem):
    z = lax.axis_index("seq_0")
    y = lax.axis_index("seq_1")
    c = lax.axis_index("seq_2")
    x = lax.axis_index("head")
    nz = lax.axis_size("seq_0")
    place = y * 2 + c
    width = out_ref.shape[1]
    half = width // 2
    znext = lax.rem(z + 1, nz)

    pltpu.make_async_copy(w_hbm, wv, wsem).start()

    barrier = pltpu.get_barrier_semaphore()
    for d in range(1, NB):
        pl.semaphore_signal(barrier, 1, device_id=group_id(lax.rem(place + d, NB)), device_id_type=MESH)
    for d in range(1, 8):
        pl.semaphore_signal(barrier, 1, device_id={"seq_0": lax.rem(z + d, nz)}, device_id_type=MESH)
    for d in (1, 3):
        pl.semaphore_signal(barrier, 1, device_id={"head": lax.rem(x + d, 4)}, device_id_type=MESH)
    pl.semaphore_wait(barrier, NB - 1 + 7 + 2)

    own = SEG + place * ROWS
    targets = (
        (k_hbm, kcat.at[pl.ds(pl.multiple_of(own, ROWS), ROWS), :]),
        (v_hbm, vcat.at[pl.ds(pl.multiple_of(own, ROWS), ROWS), pl.ds(0, HD)]),
        (q_hbm, qh.at[rows(place), :]),
    )

    def to_head(t, chip, core):
        block = chip * 2 + core
        return pltpu.make_async_remote_copy(
            src_ref=targets[t][0].at[:, cols(block)], dst_ref=targets[t][1],
            send_sem=ss.at[t, block], recv_sem=rs.at[t, place],
            device_id={"seq_1": chip, "seq_2": core}, device_id_type=MESH)

    others = [(y, 1 - c)]
    for dy in (1, 3, 2):
        for dc in (0, 1):
            others.append((lax.rem(y + dy, 4), lax.rem(c + dc, 2)))
    for t in (0, 1):
        pltpu.make_async_copy(targets[t][0].at[:, cols(place)], targets[t][1], rs.at[t, place]).start()
    for chip, core in others:
        for t in (0, 1):
            to_head(t, chip, core).start()
    pltpu.make_async_copy(q_hbm.at[:, cols(place)], targets[2][1], rs.at[2, place]).start()
    for chip, core in others:
        to_head(2, chip, core).start()

    vcat[:, HD:] = jnp.ones((2 * SEG, HD), BF)
    terms[...] = jnp.zeros_like(terms)

    code = jnp.where(y == 0, 0 + 3 * 4 + 2 * 16 + 1 * 64,
           jnp.where(y == 1, 1 + 2 * 4 + 3 * 16 + 0 * 64,
           jnp.where(y == 2, 2 + 3 * 4 + 1 * 16 + 0 * 64, 3 + 2 * 4 + 1 * 16 + 0 * 64)))

    def nth(i):
        pair = i // 2
        power = jnp.where(pair == 0, 1, jnp.where(pair == 1, 4, jnp.where(pair == 2, 16, 64)))
        return 2 * lax.rem(code // power, 4) + 1 - lax.rem(i, 2)

    def own_k(p):
        return kcat.at[pl.ds(pl.multiple_of(SEG + p * ROWS, ROWS), ROWS), :]

    def own_v(p):
        return vcat.at[pl.ds(pl.multiple_of(SEG + p * ROWS, ROWS), ROWS), pl.ds(0, HD)]

    def pass_on(t, p):
        src = own_k(p) if t == 0 else own_v(p)
        dst = kcat.at[rows(p), :] if t == 0 else vcat.at[rows(p), pl.ds(0, HD)]
        return pltpu.make_async_remote_copy(
            src_ref=src, dst_ref=dst, send_sem=zs.at[t, p], recv_sem=zr.at[t, p],
            device_id={"seq_0": znext}, device_id_type=MESH)

    def arrived(i):
        p = nth(i)
        pltpu.make_async_copy(own_k(p), own_k(p), rs.at[0, p]).wait()
        pltpu.make_async_copy(own_v(p), own_v(p), rs.at[1, p]).wait()
        return p

    def add_terms(p):
        at = pl.ds(pl.multiple_of(SEG + p * ROWS, ROWS), ROWS)
        soft = phi(kcat[at, :].astype(F32)).astype(BF)
        terms[...] += lax.dot_general(soft, vcat[at, :], (((0,), (0,)), ((), ())), preferred_element_type=F32)

    @pl.loop(0, FIRST)
    def _(i):
        p = arrived(i)
        pass_on(0, p).start()
        pass_on(1, p).start()
        add_terms(p)

    @pl.loop(FIRST, NB)
    def _(i):
        add_terms(arrived(i))

    tmsg[pl.ds(0, HD), :] = terms[:, :HD].astype(BF)
    norm = jnp.transpose(terms[:, HD:])[:8]
    norm_hi = norm.astype(BF)
    norm_lo = (norm - norm_hi.astype(F32)).astype(BF)
    tmsg[pl.ds(HD, 16), :] = jnp.concatenate([norm_hi, norm_lo], axis=0)

    def to_later(other):
        return pltpu.make_async_remote_copy(
            src_ref=tmsg, dst_ref=tin.at[z], send_sem=ts.at[other], recv_sem=tr.at[z],
            device_id={"seq_0": other}, device_id_type=MESH)

    for d in range(1, 8):
        @pl.when(z + d < nz)
        def _():
            to_later(z + d).start()

    @pl.loop(FIRST, NB)
    def _(i):
        p = nth(i)
        pass_on(0, p).start()
        pass_on(1, p).start()

    terms[...] = jnp.zeros_like(terms)

    @pl.loop(0, z)
    def _(other):
        pltpu.make_async_copy(tin.at[other], tin.at[other], tr.at[other]).wait()
        terms[:, :HD] += tin[other, pl.ds(0, HD), :].astype(F32)
        n = tin[other, pl.ds(HD, 16), :].astype(F32)
        terms[pl.ds(0, 8), HD:] += n[:8] + n[8:]

    norm_cols = jnp.transpose(jnp.broadcast_to(terms[0:1, HD:], (HD, HD)))
    full = jnp.concatenate([terms[:, :HD], norm_cols], axis=1)
    full_hi = full.astype(BF)
    mem[pl.ds(0, HD), :] = full_hi
    mem[pl.ds(HD, HD), :] = (full - full_hi.astype(F32)).astype(BF)

    gate = 1.0 / (1.0 + jnp.exp(-jnp.full((8, HD), beta_ref[place], F32)))[0:1]

    def back(j):
        return pltpu.make_async_remote_copy(
            src_ref=att_out.at[j], dst_ref=att_in.at[:, cols(place)],
            send_sem=as_.at[j], recv_sem=ar.at[place],
            device_id=group_id(j), device_id_type=MESH)

    @pl.loop(0, NB)
    def _(jj):
        j = NB - 1 - jj
        pltpu.make_async_copy(kcat.at[rows(j), :], kcat.at[rows(j), :], zr.at[0, j]).wait()
        pltpu.make_async_copy(vcat.at[rows(j), pl.ds(0, HD)], vcat.at[rows(j), pl.ds(0, HD)], zr.at[1, j]).wait()
        pltpu.make_async_copy(qh.at[rows(j), :], qh.at[rows(j), :], rs.at[2, j]).wait()
        q = qh[rows(j), :]
        row = lax.broadcasted_iota(jnp.int32, (ROWS, ROWS), 0)
        col = lax.broadcasted_iota(jnp.int32, (ROWS, ROWS), 1)
        scores, peaks, hidden = [], [], []
        for b in range(NB + 1):
            keys = kcat[pl.ds(pl.multiple_of((j + b) * ROWS, ROWS), ROWS), :]
            s = lax.dot_general(q, keys, (((1,), (1,)), ((), ())), preferred_element_type=F32)
            if b == 0:
                s = jnp.where(col > row, s, -jnp.inf)
            if b == NB:
                s = jnp.where(col <= row, s, -jnp.inf)
            peak = jnp.maximum(s[:, :HD], s[:, HD:])
            gone = (z == 0) & (j + b < NB)
            if b < NB:
                peak = jnp.where(gone, -jnp.inf, peak)
            scores.append(s)
            peaks.append(peak)
            hidden.append(gone)
        top = jnp.max(functools.reduce(jnp.maximum, peaks), axis=1, keepdims=True)
        acc = jnp.zeros((ROWS, 2 * HD), F32)
        for b in range(NB + 1):
            base = top if b == NB else jnp.where(hidden[b], jnp.inf, top)
            weights = jnp.exp2((scores[b] - base) * SCALE2).astype(BF)
            acc += jnp.dot(weights, vcat[pl.ds(pl.multiple_of((j + b) * ROWS, ROWS), ROWS), :],
                           preferred_element_type=F32)
        local = acc[:, :HD] / acc[:, HD:]
        soft = phi(q.astype(F32)).astype(BF)
        past = jnp.dot(jnp.concatenate([soft, soft], axis=1), mem[...], preferred_element_type=F32)
        from_memory = past[:, :HD] / (1.0 + past[:, HD:])
        att_out[j] = (gate * from_memory + (1.0 - gate) * local).astype(BF)

        @pl.when(j != place)
        def _():
            back(j).start()

        @pl.when(j == place)
        def _():
            pltpu.make_async_copy(att_out.at[j], att_in.at[:, cols(place)], ar.at[place]).start()

    @pl.loop(0, NB)
    def _(h):
        pltpu.make_async_copy(att_in.at[:, cols(h)], att_in.at[:, cols(h)], ar.at[h]).wait()

    pltpu.make_async_copy(w_hbm, wv, wsem).wait()

    up, down, far = lax.rem(x + 1, 4), lax.rem(x + 3, 4), lax.rem(x + 2, 4)

    def product(owner, start, size):
        at = pl.ds(pl.multiple_of(owner * width + start, HD), size)
        return jnp.dot(att_in[...], wv[:, at], preferred_element_type=F32)

    def to_x(src, dst, i, target):
        return pltpu.make_async_remote_copy(
            src_ref=src, dst_ref=dst, send_sem=xs.at[i], recv_sem=xr.at[i],
            device_id={"head": target}, device_id_type=MESH)

    copies = []

    def send(src, dst, i, target):
        copy = to_x(src, dst, i, target)
        copy.start()
        copies.append(copy)

    relay_out[0] = product(far, 0, half).astype(BF)
    send(relay_out.at[0], relay_in.at[0], 0, up)
    relay_out[1] = product(far, half, half).astype(BF)
    send(relay_out.at[1], relay_in.at[1], 1, down)
    part_out[1] = product(up, half, half).astype(BF)
    send(part_out.at[1], part_in.at[1], 2, up)
    part_out[2] = product(down, 0, half).astype(BF)
    send(part_out.at[2], part_in.at[2], 3, down)
    first = product(up, 0, half)
    copies[0].wait_recv()
    part_out[0] = (first + relay_in[0].astype(F32)).astype(BF)
    send(part_out.at[0], part_in.at[0], 4, up)
    second = product(down, half, half)
    copies[1].wait_recv()
    part_out[3] = (second + relay_in[1].astype(F32)).astype(BF)
    send(part_out.at[3], part_in.at[3], 5, down)
    left = product(x, 0, half)
    right = product(x, half, half)
    copies[2].wait_recv()
    copies[3].wait_recv()
    left = left + part_in[2].astype(F32)
    right = right + part_in[1].astype(F32)
    copies[4].wait_recv()
    out_ref[:, :half] = (left + part_in[0].astype(F32)).astype(BF)
    copies[5].wait_recv()
    out_ref[:, half:] = (right + part_in[3].astype(F32)).astype(BF)

    for copy in copies:
        copy.wait_send()
    for t in range(3):
        for chip, core in others:
            to_head(t, chip, core).wait_send()

    @pl.loop(0, NB)
    def _(p):
        pass_on(0, p).wait_send()
        pass_on(1, p).wait_send()

        @pl.when(p != place)
        def _():
            back(p).wait_send()

    for d in range(1, 8):
        @pl.when(z + d < nz)
        def _():
            to_later(z + d).wait_send()


def layer(queries, keys, values, beta, w_out):
    tokens, width = queries.shape
    any_space = pl.BlockSpec(memory_space=pl.ANY)
    vmem = pl.BlockSpec(memory_space=pltpu.VMEM)
    dma = pltpu.SemaphoreType.DMA
    half = width // 2
    return pl.pallas_call(
        body,
        name="infini",
        out_shape=jax.ShapeDtypeStruct((tokens, width), BF),
        in_specs=[any_space, any_space, any_space, pl.BlockSpec(memory_space=pltpu.SMEM), any_space],
        out_specs=vmem,
        scratch_shapes=[
            pltpu.VMEM((2 * SEG, HD), BF),
            pltpu.VMEM((2 * SEG, 2 * HD), BF),
            pltpu.VMEM((SEG, HD), BF),
            pltpu.VMEM(w_out.shape, BF),
            pltpu.VMEM((HD, 2 * HD), F32),
            pltpu.VMEM((HD + 16, HD), BF),
            pltpu.VMEM((8, HD + 16, HD), BF),
            pltpu.VMEM((2 * HD, 2 * HD), BF),
            pltpu.VMEM((NB, ROWS, HD), BF),
            pltpu.VMEM((ROWS, NB * HD), BF),
            pltpu.VMEM((2, tokens, half), BF),
            pltpu.VMEM((2, tokens, half), BF),
            pltpu.VMEM((4, tokens, half), BF),
            pltpu.VMEM((4, tokens, half), BF),
            dma((3, NB)), dma((3, NB)),
            dma((2, NB)), dma((2, NB)),
            dma((8,)), dma((8,)),
            dma((NB,)), dma((NB,)),
            dma((6,)), dma((6,)),
            dma(()),
        ],
        compiler_params=pltpu.CompilerParams(
            collective_id=0, has_side_effects=True, vmem_limit_bytes=56 * 1024 * 1024),
    )(queries, keys, values, beta, w_out)


def solution(mesh):
    torus = Mesh(
        mesh.devices.reshape(8, 4, 2, mesh.shape["head"]), ("seq_0", "seq_1", "seq_2", "head")
    )
    return jax.shard_map(
        layer,
        mesh=torus,
        in_specs=(P(SEQ, "head"), P(SEQ, "head"), P(SEQ, "head"), P("head"), P("head", None)),
        out_specs=P(SEQ, "head"),
        check_vma=False,
    )
```

time: 322 us -> 73.1 us (0.23)
  the two profiles are of different devices: /device:TPU:160 before, /device:TPU:96 now
where the time goes in v1:
time: 73.1 us; the launch traced here: 72.9 us
  Pallas kernels  71 us (97%)
  local copies, waits for them, and re-layouts  1.87 us (3%)
    pallas_call x1, Pallas kernels, layer(): pl.pallas_call(body, name='infini', out_shape=jax.ShapeDtypeStruct((token...  71 us
    unnamed x1, local copies, waits for them, and re-layouts  1.87 us

profile of v1, /device:TPU:96, one launch (start us, length us, event | category | flops | bytes accessed | tf_op | source)
XLA Modules:
  0.0 72.9 jit_solution(8562408031453843810)
XLA Ops:
  0.0 71.0 %infini.1 = bf16[256,1024]{1,0:T(8,128)(2,1)} custom-call(bf16[256,1024]{1,0:T(8,128)(2,1)} %q_hbm.1, bf16[256,1024]{1,0:T(8,128)(2,1)} %k_hbm.1, bf16[256,1024]{1,0:T(8,128)(2,1)} %v_hbm.1, f32[8]{0:T(128)} %beta_ref.1, bf16[1024,4096]{1,0:T(8,128)(2,1)} %w_hbm.1), custom_call_target="tpu_custom_call" | custom-call | tf_op jit(solution)/shard_map/infini/pallas_call | solution.py:306
  71.1 1.9 %copy.7 = bf16[256,1024]{1,0:T(8,128)(2,1)} copy(bf16[256,1024]{1,0:T(8,128)(2,1)} %infini.1) | data formatting | bytes 1048576

commit v2 on v1

v2 whole, which is shorter than its diff:
```python
import functools

import jax
import jax.numpy as jnp
from jax import lax
from jax.experimental import pallas as pl
from jax.experimental.pallas import tpu as pltpu
from jax.sharding import Mesh
from jax.sharding import PartitionSpec as P

HD = 128
ROWS = 256
NB = 8
SEG = NB * ROWS
SEQ = ("seq_0", "seq_1", "seq_2")
MESH = pl.DeviceIdType.MESH
BF = jnp.bfloat16
F32 = jnp.float32
SCALE2 = (HD ** -0.5) * 1.4426950408889634
GROUP = 2 * ROWS
GATE_A = 7
GATE_B = 3


def rows(block):
    return pl.ds(pl.multiple_of(block * ROWS, ROWS), ROWS)


def cols(head):
    return pl.ds(pl.multiple_of(head * HD, HD), HD)


def group_id(block):
    return {"seq_1": block // 2, "seq_2": block % 2}


def phi(x):
    return jnp.where(x > 0, x + 1.0, jnp.exp(jnp.minimum(x, 0.0)))


def body(q_hbm, k_hbm, v_hbm, beta_ref, w_hbm, out_ref,
         kcat, vcat, qh, wv, terms, tmsg, tsum, tin, past, mem, top, acc, att_out, att_in,
         relay_out, relay_in, part_out, part_in, staged,
         go, ok, ss, rs, zs, zr, ts, tr, as_, ar, xs, xr, wsem, stage_sem):
    z = lax.axis_index("seq_0")
    y = lax.axis_index("seq_1")
    c = lax.axis_index("seq_2")
    x = lax.axis_index("head")
    place = y * 2 + c
    width = out_ref.shape[1]
    half = width // 2
    quad = lax.rem(z, 4)

    stages = [pltpu.make_async_copy(src, staged.at[i], stage_sem.at[i]) for i, src in enumerate((k_hbm, v_hbm, q_hbm))]
    for copy in stages:
        copy.start()
    pltpu.make_async_copy(w_hbm, wv, wsem).start()

    barrier = pltpu.get_barrier_semaphore()
    is_a, is_b = place == GATE_A, place == GATE_B
    for d in range(1, NB):
        other = lax.rem(place + d, NB)

        @pl.when((other != GATE_A) & (other != GATE_B))
        def _():
            pl.semaphore_signal(barrier, 1, device_id=group_id(other), device_id_type=MESH)

    @pl.when(jnp.logical_not(is_a | is_b))
    def _():
        pl.semaphore_wait(barrier, NB - 1)

    @pl.when((place == GATE_A - 1) | (place == GATE_B - 1))
    def _():
        pl.semaphore_signal(go, 1, device_id=group_id(place + 1), device_id_type=MESH)

    @pl.when(is_a | is_b)
    def _():
        pl.semaphore_wait(go, 1)

    @pl.when(is_a)
    def _():
        @pl.when(z > 0)
        def _():
            pl.semaphore_signal(barrier, 1, device_id={"seq_0": z - 1}, device_id_type=MESH)

        for d in (1, 3):
            pl.semaphore_signal(barrier, 1, device_id={"head": lax.rem(x + d, 4)}, device_id_type=MESH)

    @pl.when(is_b)
    def _():
        for d in (1, 2, 3):
            @pl.when(quad >= d)
            def _():
                pl.semaphore_signal(barrier, 1, device_id={"seq_0": z - d}, device_id_type=MESH)

        @pl.when(z > 3)
        def _():
            pl.semaphore_signal(barrier, 1, device_id={"seq_0": 3}, device_id_type=MESH)

    def pass_word(i, here):
        for d in range(1, NB):
            pl.semaphore_signal(ok.at[i], 1, device_id=group_id(lax.rem(here + d, NB)), device_id_type=MESH)

    own = SEG + place * ROWS
    targets = (
        (staged.at[0], kcat.at[pl.ds(pl.multiple_of(own, ROWS), ROWS), :]),
        (staged.at[1], vcat.at[pl.ds(pl.multiple_of(own, ROWS), ROWS), pl.ds(0, HD)]),
        (staged.at[2], qh.at[rows(place), :]),
    )

    def to_head(t, chip, core):
        block = chip * 2 + core
        return pltpu.make_async_remote_copy(
            src_ref=targets[t][0].at[:, cols(block)], dst_ref=targets[t][1],
            send_sem=ss.at[t, block], recv_sem=rs.at[t, place],
            device_id={"seq_1": chip, "seq_2": core}, device_id_type=MESH)

    others = [(y, 1 - c)]
    for dy in (1, 3, 2):
        for dc in (0, 1):
            others.append((lax.rem(y + dy, 4), lax.rem(c + dc, 2)))
    for t in (0, 1):
        pltpu.make_async_copy((k_hbm, v_hbm)[t].at[:, cols(place)], targets[t][1], rs.at[t, place]).start()
    stages[0].wait()
    stages[1].wait()
    for chip, core in others:
        for t in (0, 1):
            to_head(t, chip, core).start()
    pltpu.make_async_copy(q_hbm.at[:, cols(place)], targets[2][1], rs.at[2, place]).start()
    stages[2].wait()
    for chip, core in others:
        to_head(2, chip, core).start()

    vcat[:, HD:] = jnp.ones((2 * SEG, HD), BF)
    terms[...] = jnp.zeros_like(terms)

    code = jnp.where(y == 0, 0 + 3 * 4 + 2 * 16 + 1 * 64,
           jnp.where(y == 1, 1 + 2 * 4 + 3 * 16 + 0 * 64,
           jnp.where(y == 2, 2 + 3 * 4 + 1 * 16 + 0 * 64, 3 + 2 * 4 + 1 * 16 + 0 * 64)))

    def nth(i):
        pair = i // 2
        power = jnp.where(pair == 0, 1, jnp.where(pair == 1, 4, jnp.where(pair == 2, 16, 64)))
        return 2 * lax.rem(code // power, 4) + 1 - lax.rem(i, 2)

    def own_k(p):
        return kcat.at[pl.ds(pl.multiple_of(SEG + p * ROWS, ROWS), ROWS), :]

    def own_v(p):
        return vcat.at[pl.ds(pl.multiple_of(SEG + p * ROWS, ROWS), ROWS), pl.ds(0, HD)]

    def pass_on(t, p):
        src = own_k(p) if t == 0 else own_v(p)
        dst = kcat.at[rows(p), :] if t == 0 else vcat.at[rows(p), pl.ds(0, HD)]
        return pltpu.make_async_remote_copy(
            src_ref=src, dst_ref=dst, send_sem=zs.at[t, p], recv_sem=zr.at[t, p],
            device_id={"seq_0": z + 1}, device_id_type=MESH)

    def arrived(i):
        p = nth(i)
        pltpu.make_async_copy(own_k(p), own_k(p), rs.at[0, p]).wait()
        pltpu.make_async_copy(own_v(p), own_v(p), rs.at[1, p]).wait()
        return p

    def add_terms(p):
        at = pl.ds(pl.multiple_of(SEG + p * ROWS, ROWS), ROWS)
        soft = phi(kcat[at, :].astype(F32)).astype(BF)
        terms[...] += lax.dot_general(soft, vcat[at, :], (((0,), (0,)), ((), ())), preferred_element_type=F32)

    @pl.when(is_a)
    def _():
        pl.semaphore_wait(barrier, jnp.where(z < 7, 3, 2))
        pass_word(0, GATE_A)

    @pl.when(jnp.logical_not(is_a))
    def _():
        pl.semaphore_wait(ok.at[0], 1)

    def forward(p):
        @pl.when(z < 7)
        def _():
            pass_on(0, p).start()
            pass_on(1, p).start()

    @pl.loop(0, 4)
    def _(i):
        p = arrived(i)
        forward(p)
        add_terms(p)

    @pl.loop(4, NB)
    def _(i):
        add_terms(arrived(i))

    hears = 3 - quad + jnp.where(z == 3, 4, 0)

    @pl.when(is_b)
    def _():
        @pl.when(hears > 0)
        def _():
            pl.semaphore_wait(barrier, hears)

        pass_word(1, GATE_B)

    @pl.when(jnp.logical_not(is_b))
    def _():
        pl.semaphore_wait(ok.at[1], 1)

    def put(dst, block, norm):
        dst[pl.ds(0, HD), :] = block.astype(BF)
        norm_hi = norm.astype(BF)
        norm_lo = (norm - norm_hi.astype(F32)).astype(BF)
        dst[pl.ds(HD, 16), :] = jnp.concatenate([norm_hi, norm_lo], axis=0)

    def add_in(slot):
        pltpu.make_async_copy(tin.at[slot], tin.at[slot], tr.at[slot]).wait()
        past[:, :HD] += tin[slot, pl.ds(0, HD), :].astype(F32)
        n = tin[slot, pl.ds(HD, 16), :].astype(F32)
        past[pl.ds(0, 8), HD:] += n[:8] + n[8:]

    def to_quad(d):
        return pltpu.make_async_remote_copy(
            src_ref=tmsg, dst_ref=tin.at[quad], send_sem=ts.at[d], recv_sem=tr.at[quad],
            device_id={"seq_0": z + d}, device_id_type=MESH)

    def to_upper(d):
        return pltpu.make_async_remote_copy(
            src_ref=tsum, dst_ref=tin.at[4], send_sem=ts.at[3 + d], recv_sem=tr.at[4],
            device_id={"seq_0": z + d}, device_id_type=MESH)

    norm_rows = jnp.transpose(terms[:, HD:])[:8]
    put(tmsg, terms[:, :HD], norm_rows)
    past[...] = jnp.zeros_like(past)
    for d in (1, 2, 3):
        @pl.when(quad + d < 4)
        def _():
            to_quad(d).start()

    @pl.loop(4, 6)
    def _(i):
        forward(nth(i))

    @pl.when(z == 3)
    def _():
        for slot in range(3):
            add_in(slot)
        put(tsum, past[:, :HD] + terms[:, :HD], past[pl.ds(0, 8), HD:] + jnp.transpose(terms[:, HD:])[:8])
        for d in (1, 2, 3, 4):
            to_upper(d).start()

    @pl.loop(6, NB)
    def _(i):
        forward(nth(i))

    gate = 1.0 / (1.0 + jnp.exp(-jnp.full((8, HD), beta_ref[place], F32)))[0:1]

    def back(j):
        return pltpu.make_async_remote_copy(
            src_ref=att_out.at[rows(j), :], dst_ref=att_in.at[:, cols(place)],
            send_sem=as_.at[j], recv_sem=ar.at[place],
            device_id=group_id(j), device_id_type=MESH)

    row = lax.broadcasted_iota(jnp.int32, (ROWS, ROWS), 0)
    col = lax.broadcasted_iota(jnp.int32, (ROWS, ROWS), 1)

    def at_rows(start):
        return pl.ds(pl.multiple_of(start, ROWS), ROWS)

    def meet(*jobs):
        held = [None] * len(jobs)

        def score(n):
            j, blocks, first = jobs[n]
            q = qh[rows(j), :]
            old = None if first else top[rows(j), :]
            scores = []
            for start, mask in blocks:
                s = lax.dot_general(q, kcat[at_rows(start), :], (((1,), (1,)), ((), ())), preferred_element_type=F32)
                if mask == "le":
                    s = jnp.where(col <= row, s, -jnp.inf)
                elif mask == "gt":
                    s = jnp.where(col > row, s, -jnp.inf)
                scores.append(s)
            held[n] = (old, scores)

        def soften(n):
            old, scores = held[n]
            peak = functools.reduce(jnp.maximum, [s[:, i * HD:(i + 1) * HD] for s in scores for i in (0, 1)])
            peak = jnp.broadcast_to(jnp.max(peak, axis=1, keepdims=True), (ROWS, HD))
            fade = None
            if old is not None:
                peak = jnp.maximum(old, peak)
                fade = jnp.exp2((old - peak) * SCALE2)
            both = jnp.concatenate([peak, peak], axis=1)
            held[n] = (peak, fade, [jnp.exp2((s - both) * SCALE2).astype(BF) for s in scores])

        def gather(n):
            j, blocks, _ = jobs[n]
            peak, fade, weights = held[n]
            out = None
            for w, (start, _) in zip(weights, blocks):
                more = jnp.dot(w, vcat[at_rows(start), :], preferred_element_type=F32)
                out = more if out is None else out + more
            if fade is not None:
                out = acc[rows(j), :] * jnp.concatenate([fade, fade], axis=1) + out
            acc[rows(j), :] = out
            held[n] = peak

        for n in range(len(jobs) + 2):
            if n < len(jobs):
                score(n)
            if 0 <= n - 1 < len(jobs):
                soften(n - 1)
            if n >= 2:
                gather(n - 2)
        for (j, _, _), peak in zip(jobs, held):
            top[rows(j), :] = peak

    def own_diagonal(g):
        base = SEG + g * GROUP
        return [(2 * g, [(base, "le")], True), (2 * g + 1, [(base, None), (base + ROWS, "le")], True)]

    def whole(g, base):
        return [(2 * g + i, [(base, None), (base + ROWS, None)], False) for i in (0, 1)]

    def previous_diagonal(g):
        base = g * GROUP
        return [(2 * g, [(base, "gt"), (base + ROWS, None)], False), (2 * g + 1, [(base + ROWS, "gt")], False)]

    @pl.loop(0, 2)
    def _(i):
        for k in range(4):
            j = 4 * i + k
            pltpu.make_async_copy(qh.at[rows(j), :], qh.at[rows(j), :], rs.at[2, j]).wait()
        meet(*own_diagonal(2 * i), *own_diagonal(2 * i + 1))

    @pl.loop(0, 3)
    def _(i):
        meet(*whole(3, SEG + i * GROUP), *whole(jnp.minimum(1 + i, 2), SEG + jnp.maximum(i - 1, 0) * GROUP))

    @pl.when(z != 3)
    def _():
        @pl.loop(0, quad)
        def _(slot):
            add_in(slot)

        @pl.when(z > 3)
        def _():
            add_in(4)

    norm_cols = jnp.transpose(jnp.broadcast_to(past[0:1, HD:], (HD, HD)))
    full = jnp.concatenate([past[:, :HD], norm_cols], axis=1)
    full_hi = full.astype(BF)
    mem[pl.ds(0, HD), :] = full_hi
    mem[pl.ds(HD, HD), :] = (full - full_hi.astype(F32)).astype(BF)

    def finish(j):
        local = acc[rows(j), :HD] / acc[rows(j), HD:]
        soft = phi(qh[rows(j), :].astype(F32)).astype(BF)
        found = jnp.dot(jnp.concatenate([soft, soft], axis=1), mem[...], preferred_element_type=F32)
        from_memory = found[:, :HD] / (1.0 + found[:, HD:])
        att_out[rows(j), :] = (gate * from_memory + (1.0 - gate) * local).astype(BF)

        @pl.when(j != place)
        def _():
            back(j).start()

        @pl.when(j == place)
        def _():
            pltpu.make_async_copy(att_out.at[rows(j), :], att_in.at[:, cols(place)], ar.at[place]).start()

    complete = jnp.where(y == 0, 3 + 3 * 4 + 2 * 16 + 1 * 64,
               jnp.where(y == 1, 3 + 2 * 4 + 2 * 16 + 2 * 64,
               jnp.where(y == 2, 3 + 2 * 4 + 1 * 16 + 1 * 64, 3 + 2 * 4 + 1 * 16 + 0 * 64)))

    @pl.loop(0, 4)
    def _(i):
        g = nth(2 * i) // 2

        @pl.when(z > 0)
        def _():
            for j in (2 * g, 2 * g + 1):
                pltpu.make_async_copy(kcat.at[rows(j), :], kcat.at[rows(j), :], zr.at[0, j]).wait()
                pltpu.make_async_copy(vcat.at[rows(j), pl.ds(0, HD)], vcat.at[rows(j), pl.ds(0, HD)], zr.at[1, j]).wait()

            @pl.when(g == 0)
            def _():
                meet(*previous_diagonal(0))

            @pl.when(g > 0)
            def _():
                meet(*previous_diagonal(g), *whole(0, g * GROUP))

            @pl.when(g == 2)
            def _():
                meet(*whole(1, 2 * GROUP))

            @pl.when(g == 3)
            def _():
                meet(*whole(1, 3 * GROUP), *whole(2, 3 * GROUP))

        @pl.loop(0, NB)
        def _(jj):
            j = NB - 1 - jj
            pair = j // 2
            power = jnp.where(pair == 0, 1, jnp.where(pair == 1, 4, jnp.where(pair == 2, 16, 64)))

            @pl.when(lax.rem(complete // power, 4) == i)
            def _():
                finish(j)

    @pl.loop(0, NB)
    def _(h):
        pltpu.make_async_copy(att_in.at[:, cols(h)], att_in.at[:, cols(h)], ar.at[h]).wait()

    pltpu.make_async_copy(w_hbm, wv, wsem).wait()

    up, down, far = lax.rem(x + 1, 4), lax.rem(x + 3, 4), lax.rem(x + 2, 4)

    def product(owner, start, size):
        at = pl.ds(pl.multiple_of(owner * width + start, HD), size)
        return jnp.dot(att_in[...], wv[:, at], preferred_element_type=F32)

    def to_x(src, dst, i, target):
        return pltpu.make_async_remote_copy(
            src_ref=src, dst_ref=dst, send_sem=xs.at[i], recv_sem=xr.at[i],
            device_id={"head": target}, device_id_type=MESH)

    copies = []

    def send(src, dst, i, target):
        copy = to_x(src, dst, i, target)
        copy.start()
        copies.append(copy)

    relay_out[0] = product(far, 0, half).astype(BF)
    send(relay_out.at[0], relay_in.at[0], 0, up)
    relay_out[1] = product(far, half, half).astype(BF)
    send(relay_out.at[1], relay_in.at[1], 1, down)
    part_out[1] = product(up, half, half).astype(BF)
    send(part_out.at[1], part_in.at[1], 2, up)
    part_out[2] = product(down, 0, half).astype(BF)
    send(part_out.at[2], part_in.at[2], 3, down)
    first = product(up, 0, half)
    copies[0].wait_recv()
    part_out[0] = (first + relay_in[0].astype(F32)).astype(BF)
    send(part_out.at[0], part_in.at[0], 4, up)
    second = product(down, half, half)
    copies[1].wait_recv()
    part_out[3] = (second + relay_in[1].astype(F32)).astype(BF)
    send(part_out.at[3], part_in.at[3], 5, down)
    left = product(x, 0, half)
    right = product(x, half, half)
    copies[2].wait_recv()
    copies[3].wait_recv()
    left = left + part_in[2].astype(F32)
    right = right + part_in[1].astype(F32)
    copies[4].wait_recv()
    out_ref[:, :half] = (left + part_in[0].astype(F32)).astype(BF)
    copies[5].wait_recv()
    out_ref[:, half:] = (right + part_in[3].astype(F32)).astype(BF)

    for copy in copies:
        copy.wait_send()
    for t in range(3):
        for chip, core in others:
            to_head(t, chip, core).wait_send()

    @pl.loop(0, NB)
    def _(p):
        @pl.when(z < 7)
        def _():
            pass_on(0, p).wait_send()
            pass_on(1, p).wait_send()

        @pl.when(p != place)
        def _():
            back(p).wait_send()

    for d in (1, 2, 3):
        @pl.when(quad + d < 4)
        def _():
            to_quad(d).wait_send()

    @pl.when(z == 3)
    def _():
        for d in (1, 2, 3, 4):
            to_upper(d).wait_send()


def layer(queries, keys, values, beta, w_out):
    tokens, width = queries.shape
    any_space = pl.BlockSpec(memory_space=pl.ANY)
    vmem = pl.BlockSpec(memory_space=pltpu.VMEM)
    dma = pltpu.SemaphoreType.DMA
    half = width // 2
    return pl.pallas_call(
        body,
        name="infini",
        out_shape=jax.ShapeDtypeStruct((tokens, width), BF),
        in_specs=[any_space, any_space, any_space, pl.BlockSpec(memory_space=pltpu.SMEM), any_space],
        out_specs=vmem,
        scratch_shapes=[
            pltpu.VMEM((2 * SEG, HD), BF),
            pltpu.VMEM((2 * SEG, 2 * HD), BF),
            pltpu.VMEM((SEG, HD), BF),
            pltpu.VMEM(w_out.shape, BF),
            pltpu.VMEM((HD, 2 * HD), F32),
            pltpu.VMEM((HD + 16, HD), BF),
            pltpu.VMEM((HD + 16, HD), BF),
            pltpu.VMEM((5, HD + 16, HD), BF),
            pltpu.VMEM((HD, 2 * HD), F32),
            pltpu.VMEM((2 * HD, 2 * HD), BF),
            pltpu.VMEM((SEG, HD), F32),
            pltpu.VMEM((SEG, 2 * HD), F32),
            pltpu.VMEM((SEG, HD), BF),
            pltpu.VMEM((ROWS, NB * HD), BF),
            pltpu.VMEM((2, tokens, half), BF),
            pltpu.VMEM((2, tokens, half), BF),
            pltpu.VMEM((4, tokens, half), BF),
            pltpu.VMEM((4, tokens, half), BF),
            pltpu.VMEM((3, tokens, width), BF),
            pltpu.SemaphoreType.REGULAR, pltpu.SemaphoreType.REGULAR((2,)),
            dma((3, NB)), dma((3, NB)),
            dma((2, NB)), dma((2, NB)),
            dma((8,)), dma((8,)),
            dma((NB,)), dma((NB,)),
            dma((6,)), dma((6,)),
            dma(()), dma((3,)),
        ],
        compiler_params=pltpu.CompilerParams(
            collective_id=0, has_side_effects=True, vmem_limit_bytes=56 * 1024 * 1024),
    )(queries, keys, values, beta, w_out)


def solution(mesh):
    torus = Mesh(
        mesh.devices.reshape(8, 4, 2, mesh.shape["head"]), ("seq_0", "seq_1", "seq_2", "head")
    )
    return jax.shard_map(
        layer,
        mesh=torus,
        in_specs=(P(SEQ, "head"), P(SEQ, "head"), P(SEQ, "head"), P("head"), P("head", None)),
        out_specs=P(SEQ, "head"),
        check_vma=False,
    )
```

time: 73.1 us -> 69.2 us (0.947)
  the two profiles are of different devices: /device:TPU:96 before, /device:TPU:160 now
where the time goes in v2:
time: 69.2 us; the launch traced here: 69.1 us
  Pallas kernels  67.2 us (97%)
  local copies, waits for them, and re-layouts  1.87 us (3%)
    pallas_call x1, Pallas kernels, layer(): pl.pallas_call(body, name='infini', out_shape=jax.ShapeDtypeStruct((token...  67.2 us
    unnamed x1, local copies, waits for them, and re-layouts  1.87 us

profile of v2, /device:TPU:160, one launch (start us, length us, event | category | flops | bytes accessed | tf_op | source)
XLA Modules:
  0.0 69.1 jit_solution(14039961343392374247)
XLA Ops:
  0.0 67.2 %infini.1 = bf16[256,1024]{1,0:T(8,128)(2,1)} custom-call(bf16[256,1024]{1,0:T(8,128)(2,1)} %q_hbm.1, bf16[256,1024]{1,0:T(8,128)(2,1)} %k_hbm.1, bf16[256,1024]{1,0:T(8,128)(2,1)} %v_hbm.1, f32[8]{0:T(128)} %beta_ref.1, bf16[1024,4096]{1,0:T(8,128)(2,1)} %w_hbm.1), custom_call_target="tpu_custom_call" | custom-call | tf_op jit(solution)/shard_map/infini/pallas_call | solution.py:497
  67.2 1.9 %copy.7 = bf16[256,1024]{1,0:T(8,128)(2,1)} copy(bf16[256,1024]{1,0:T(8,128)(2,1)} %infini.1) | data formatting | bytes 1048576

commit v3 on v2

--- a/solution.py
+++ b/solution.py
@@ -18,16 +18,18 @@
 F32 = jnp.float32
 SCALE2 = (HD ** -0.5) * 1.4426950408889634
 GROUP = 2 * ROWS
-GATE_A = 7
-GATE_B = 3
+
+
+def aligned(start, size):
+    return start if isinstance(start, int) else pl.multiple_of(start, size)
 
 
 def rows(block):
-    return pl.ds(pl.multiple_of(block * ROWS, ROWS), ROWS)
+    return pl.ds(aligned(block * ROWS, ROWS), ROWS)
 
 
 def cols(head):
-    return pl.ds(pl.multiple_of(head * HD, HD), HD)
+    return pl.ds(aligned(head * HD, HD), HD)
 
 
 def group_id(block):
@@ -41,7 +43,7 @@
 def body(q_hbm, k_hbm, v_hbm, beta_ref, w_hbm, out_ref,
          kcat, vcat, qh, wv, terms, tmsg, tsum, tin, past, mem, top, acc, att_out, att_in,
          relay_out, relay_in, part_out, part_in, staged,
-         go, ok, ss, rs, zs, zr, ts, tr, as_, ar, xs, xr, wsem, stage_sem):
+         go, ok, up, ss, rs, zs, zr, ts, tr, as_, ar, xs, xr, wsem, stage_sem):
     z = lax.axis_index("seq_0")
     y = lax.axis_index("seq_1")
     c = lax.axis_index("seq_2")
@@ -57,49 +59,45 @@
     pltpu.make_async_copy(w_hbm, wv, wsem).start()
 
     barrier = pltpu.get_barrier_semaphore()
-    is_a, is_b = place == GATE_A, place == GATE_B
     for d in range(1, NB):
         other = lax.rem(place + d, NB)
 
-        @pl.when((other != GATE_A) & (other != GATE_B))
+        @pl.when(lax.rem(other, 2) == 0)
         def _():
             pl.semaphore_signal(barrier, 1, device_id=group_id(other), device_id_type=MESH)
 
-    @pl.when(jnp.logical_not(is_a | is_b))
+    @pl.when(c == 0)
     def _():
         pl.semaphore_wait(barrier, NB - 1)
-
-    @pl.when((place == GATE_A - 1) | (place == GATE_B - 1))
-    def _():
-        pl.semaphore_signal(go, 1, device_id=group_id(place + 1), device_id_type=MESH)
-
-    @pl.when(is_a | is_b)
+        pl.semaphore_signal(go, 1, device_id={"seq_2": 1}, device_id_type=MESH)
+
+    @pl.when(c == 1)
     def _():
         pl.semaphore_wait(go, 1)
 
-    @pl.when(is_a)
-    def _():
         @pl.when(z > 0)
         def _():
             pl.semaphore_signal(barrier, 1, device_id={"seq_0": z - 1}, device_id_type=MESH)
+
+        @pl.when(z < 7)
+        def _():
+            pl.semaphore_signal(barrier, 1, device_id={"seq_0": z + 1}, device_id_type=MESH)
 
         for d in (1, 3):
             pl.semaphore_signal(barrier, 1, device_id={"head": lax.rem(x + d, 4)}, device_id_type=MESH)
 
-    @pl.when(is_b)
-    def _():
-        for d in (1, 2, 3):
-            @pl.when(quad >= d)
-            def _():
-                pl.semaphore_signal(barrier, 1, device_id={"seq_0": z - d}, device_id_type=MESH)
-
-        @pl.when(z > 3)
-        def _():
-            pl.semaphore_signal(barrier, 1, device_id={"seq_0": 3}, device_id_type=MESH)
-
-    def pass_word(i, here):
-        for d in range(1, NB):
-            pl.semaphore_signal(ok.at[i], 1, device_id=group_id(lax.rem(here + d, NB)), device_id_type=MESH)
+    def pass_word(i):
+        pl.semaphore_signal(ok.at[i], 1, device_id={"seq_2": 0}, device_id_type=MESH)
+
+    def hear_of(i):
+        @pl.when((c == 1) & (z <= 5 - i))
+        def _():
+            pl.semaphore_wait(up.at[i], 1)
+
+            if i < 2:
+                @pl.when(z > 0)
+                def _():
+                    pl.semaphore_signal(up.at[i + 1], 1, device_id={"seq_0": z - 1}, device_id_type=MESH)
 
     own = SEG + place * ROWS
     targets = (
@@ -123,13 +121,25 @@
         pltpu.make_async_copy((k_hbm, v_hbm)[t].at[:, cols(place)], targets[t][1], rs.at[t, place]).start()
     stages[0].wait()
     stages[1].wait()
-    for chip, core in others:
+    for chip, core in others[:5]:
         for t in (0, 1):
             to_head(t, chip, core).start()
     pltpu.make_async_copy(q_hbm.at[:, cols(place)], targets[2][1], rs.at[2, place]).start()
     stages[2].wait()
-    for chip, core in others:
-        to_head(2, chip, core).start()
+    to_head(2, y, 1 - c).start()
+
+    @pl.when(c == 1)
+    def _():
+        pl.semaphore_wait(barrier, 2 + jnp.where(z < 7, 1, 0) + jnp.where(z > 0, 1, 0))
+        pass_word(0)
+
+        @pl.when((z > 0) & (z < 7))
+        def _():
+            pl.semaphore_signal(up.at[0], 1, device_id={"seq_0": z - 1}, device_id_type=MESH)
+
+    @pl.when(c == 0)
+    def _():
+        pl.semaphore_wait(ok.at[0], 1)
 
     vcat[:, HD:] = jnp.ones((2 * SEG, HD), BF)
     terms[...] = jnp.zeros_like(terms)
@@ -167,42 +177,44 @@
         soft = phi(kcat[at, :].astype(F32)).astype(BF)
         terms[...] += lax.dot_general(soft, vcat[at, :], (((0,), (0,)), ((), ())), preferred_element_type=F32)
 
-    @pl.when(is_a)
-    def _():
-        pl.semaphore_wait(barrier, jnp.where(z < 7, 3, 2))
-        pass_word(0, GATE_A)
-
-    @pl.when(jnp.logical_not(is_a))
-    def _():
-        pl.semaphore_wait(ok.at[0], 1)
-
     def forward(p):
         @pl.when(z < 7)
         def _():
             pass_on(0, p).start()
             pass_on(1, p).start()
 
-    @pl.loop(0, 4)
+    @pl.loop(0, 2)
     def _(i):
         p = arrived(i)
         forward(p)
         add_terms(p)
 
+    for chip, core in others[5:]:
+        for t in (0, 1):
+            to_head(t, chip, core).start()
+    hear_of(0)
+
+    @pl.loop(2, 4)
+    def _(i):
+        p = arrived(i)
+        forward(p)
+        add_terms(p)
+
+    for chip, core in others[1:]:
+        to_head(2, chip, core).start()
+    hear_of(1)
+
     @pl.loop(4, NB)
     def _(i):
         add_terms(arrived(i))
 
-    hears = 3 - quad + jnp.where(z == 3, 4, 0)
-
-    @pl.when(is_b)
-    def _():
-        @pl.when(hears > 0)
-        def _():
-            pl.semaphore_wait(barrier, hears)
-
-        pass_word(1, GATE_B)
-
-    @pl.when(jnp.logical_not(is_b))
+    hear_of(2)
+
+    @pl.when(c == 1)
+    def _():
+        pass_word(1)
+
+    @pl.when(c == 0)
     def _():
         pl.semaphore_wait(ok.at[1], 1)
 
@@ -240,18 +252,6 @@
     def _(i):
         forward(nth(i))
 
-    @pl.when(z == 3)
-    def _():
-        for slot in range(3):
-            add_in(slot)
-        put(tsum, past[:, :HD] + terms[:, :HD], past[pl.ds(0, 8), HD:] + jnp.transpose(terms[:, HD:])[:8])
-        for d in (1, 2, 3, 4):
-            to_upper(d).start()
-
-    @pl.loop(6, NB)
-    def _(i):
-        forward(nth(i))
-
     gate = 1.0 / (1.0 + jnp.exp(-jnp.full((8, HD), beta_ref[place], F32)))[0:1]
 
     def back(j):
@@ -264,7 +264,7 @@
     col = lax.broadcasted_iota(jnp.int32, (ROWS, ROWS), 1)
 
     def at_rows(start):
-        return pl.ds(pl.multiple_of(start, ROWS), ROWS)
+        return pl.ds(aligned(start, ROWS), ROWS)
 
     def meet(*jobs):
         held = [None] * len(jobs)
@@ -316,10 +316,6 @@
         for (j, _, _), peak in zip(jobs, held):
             top[rows(j), :] = peak
 
-    def own_diagonal(g):
-        base = SEG + g * GROUP
-        return [(2 * g, [(base, "le")], True), (2 * g + 1, [(base, None), (base + ROWS, "le")], True)]
-
     def whole(g, base):
         return [(2 * g + i, [(base, None), (base + ROWS, None)], False) for i in (0, 1)]
 
@@ -327,32 +323,34 @@
         base = g * GROUP
         return [(2 * g, [(base, "gt"), (base + ROWS, None)], False), (2 * g + 1, [(base + ROWS, "gt")], False)]
 
-    @pl.loop(0, 2)
+    near = jnp.where(y == 0, 0 + 3 * 4 + 1 * 16 + 2 * 64,
+           jnp.where(y == 1, 1 + 2 * 4 + 0 * 16 + 3 * 64,
+           jnp.where(y == 2, 2 + 3 * 4 + 1 * 16 + 0 * 64, 3 + 2 * 4 + 0 * 16 + 1 * 64)))
+
+    @pl.loop(0, 4)
     def _(i):
-        for k in range(4):
-            j = 4 * i + k
+        power = jnp.where(i == 0, 1, jnp.where(i == 1, 4, jnp.where(i == 2, 16, 64)))
+        g = lax.rem(near // power, 4)
+        for j in (2 * g, 2 * g + 1):
             pltpu.make_async_copy(qh.at[rows(j), :], qh.at[rows(j), :], rs.at[2, j]).wait()
-        meet(*own_diagonal(2 * i), *own_diagonal(2 * i + 1))
-
-    @pl.loop(0, 3)
-    def _(i):
-        meet(*whole(3, SEG + i * GROUP), *whole(jnp.minimum(1 + i, 2), SEG + jnp.maximum(i - 1, 0) * GROUP))
-
-    @pl.when(z != 3)
-    def _():
-        @pl.loop(0, quad)
-        def _(slot):
-            add_in(slot)
-
-        @pl.when(z > 3)
-        def _():
-            add_in(4)
-
-    norm_cols = jnp.transpose(jnp.broadcast_to(past[0:1, HD:], (HD, HD)))
-    full = jnp.concatenate([past[:, :HD], norm_cols], axis=1)
-    full_hi = full.astype(BF)
-    mem[pl.ds(0, HD), :] = full_hi
-    mem[pl.ds(HD, HD), :] = (full - full_hi.astype(F32)).astype(BF)
+        for own_g in range(4):
+            @pl.when(g == own_g)
+            def _():
+                meet(*[(j, [(SEG + k * ROWS, None) for k in range(j)] + [(SEG + j * ROWS, "le")], True)
+                       for j in (2 * own_g, 2 * own_g + 1)])
+
+        @pl.when(i == 1)
+        def _():
+            @pl.when(z == 3)
+            def _():
+                for slot in range(3):
+                    add_in(slot)
+                put(tsum, past[:, :HD] + terms[:, :HD], past[pl.ds(0, 8), HD:] + jnp.transpose(terms[:, HD:])[:8])
+                for d in (1, 2, 3, 4):
+                    to_upper(d).start()
+
+            for k in (6, 7):
+                forward(nth(k))
 
     def finish(j):
         local = acc[rows(j), :HD] / acc[rows(j), HD:]
@@ -369,45 +367,73 @@
         def _():
             pltpu.make_async_copy(att_out.at[rows(j), :], att_in.at[:, cols(place)], ar.at[place]).start()
 
-    complete = jnp.where(y == 0, 3 + 3 * 4 + 2 * 16 + 1 * 64,
-               jnp.where(y == 1, 3 + 2 * 4 + 2 * 16 + 2 * 64,
-               jnp.where(y == 2, 3 + 2 * 4 + 1 * 16 + 1 * 64, 3 + 2 * 4 + 1 * 16 + 0 * 64)))
+    def came(j):
+        pltpu.make_async_copy(kcat.at[rows(j), :], kcat.at[rows(j), :], zr.at[0, j]).wait()
+        pltpu.make_async_copy(vcat.at[rows(j), pl.ds(0, HD)], vcat.at[rows(j), pl.ds(0, HD)], zr.at[1, j]).wait()
+
+    def meet_previous(g):
+        @pl.when(z > 0)
+        def _():
+            came(2 * g + 1)
+            came(2 * g)
+            jobs = previous_diagonal(g)
+            for k in range(g):
+                jobs = jobs + whole(k, g * GROUP)
+            meet(*jobs)
+
+    meet_previous(3)
+    meet_previous(2)
+
+    @pl.when(z != 3)
+    def _():
+        @pl.loop(0, quad)
+        def _(slot):
+            add_in(slot)
+
+        @pl.when(z > 3)
+        def _():
+            add_in(4)
+
+    norm_cols = jnp.transpose(jnp.broadcast_to(past[0:1, HD:], (HD, HD)))
+    full = jnp.concatenate([past[:, :HD], norm_cols], axis=1)
+    full_hi = full.astype(BF)
+    mem[pl.ds(0, HD), :] = full_hi
+    mem[pl.ds(HD, HD), :] = (full - full_hi.astype(F32)).astype(BF)
 
     @pl.loop(0, 4)
     def _(i):
-        g = nth(2 * i) // 2
+        finish(7 - i)
+
+    @pl.when(y == 0)
+    def _():
+        meet_previous(0)
+        meet_previous(1)
+
+        @pl.loop(0, 4)
+        def _(j):
+            finish(j)
+
+    @pl.when(y != 0)
+    def _():
+        meet_previous(1)
+
+        @pl.loop(2, 4)
+        def _(j):
+            finish(j)
 
         @pl.when(z > 0)
         def _():
-            for j in (2 * g, 2 * g + 1):
-                pltpu.make_async_copy(kcat.at[rows(j), :], kcat.at[rows(j), :], zr.at[0, j]).wait()
-                pltpu.make_async_copy(vcat.at[rows(j), pl.ds(0, HD)], vcat.at[rows(j), pl.ds(0, HD)], zr.at[1, j]).wait()
-
-            @pl.when(g == 0)
-            def _():
-                meet(*previous_diagonal(0))
-
-            @pl.when(g > 0)
-            def _():
-                meet(*previous_diagonal(g), *whole(0, g * GROUP))
-
-            @pl.when(g == 2)
-            def _():
-                meet(*whole(1, 2 * GROUP))
-
-            @pl.when(g == 3)
-            def _():
-                meet(*whole(1, 3 * GROUP), *whole(2, 3 * GROUP))
-
-        @pl.loop(0, NB)
-        def _(jj):
-            j = NB - 1 - jj
-            pair = j // 2
-            power = jnp.where(pair == 0, 1, jnp.where(pair == 1, 4, jnp.where(pair == 2, 16, 64)))
-
-            @pl.when(lax.rem(complete // power, 4) == i)
-            def _():
-                finish(j)
+            came(1)
+            meet((1, [(ROWS, "gt")], False), (0, [(ROWS, None)], False))
+
+        finish(1)
+
+        @pl.when(z > 0)
+        def _():
+            came(0)
+            meet((0, [(0, "gt")], False))
+
+        finish(0)
 
     @pl.loop(0, NB)
     def _(h):
@@ -520,7 +546,7 @@
             pltpu.VMEM((4, tokens, half), BF),
             pltpu.VMEM((4, tokens, half), BF),
             pltpu.VMEM((3, tokens, width), BF),
-            pltpu.SemaphoreType.REGULAR, pltpu.SemaphoreType.REGULAR((2,)),
+            pltpu.SemaphoreType.REGULAR, pltpu.SemaphoreType.REGULAR((2,)), pltpu.SemaphoreType.REGULAR((3,)),
             dma((3, NB)), dma((3, NB)),
             dma((2, NB)), dma((2, NB)),
             dma((8,)), dma((8,)),

time: 69.2 us -> 66.5 us (0.961)
  Pallas kernels: 67.2 us -> 64.5 us
    pallas_call x1, Pallas kernels: 67.2 us -> 64.5 us  [layer(): pl.pallas_call(body, name='infini', out_shape=jax.ShapeDtypeStruct((token...]
where the time goes in v3:
time: 66.5 us; the launch traced here: 66.4 us
  Pallas kernels  64.5 us (97%)
  local copies, waits for them, and re-layouts  1.87 us (3%)
    pallas_call x1, Pallas kernels, layer(): pl.pallas_call(body, name='infini', out_shape=jax.ShapeDtypeStruct((token...  64.5 us
    unnamed x1, local copies, waits for them, and re-layouts  1.87 us

profile of v3, /device:TPU:160, one launch (start us, length us, event | category | flops | bytes accessed | tf_op | source)
XLA Modules:
  0.0 66.4 jit_solution(17239050595601864321)
XLA Ops:
  0.0 64.5 %infini.1 = bf16[256,1024]{1,0:T(8,128)(2,1)} custom-call(bf16[256,1024]{1,0:T(8,128)(2,1)} %q_hbm.1, bf16[256,1024]{1,0:T(8,128)(2,1)} %k_hbm.1, bf16[256,1024]{1,0:T(8,128)(2,1)} %v_hbm.1, f32[8]{0:T(128)} %beta_ref.1, bf16[1024,4096]{1,0:T(8,128)(2,1)} %w_hbm.1), custom_call_target="tpu_custom_call" | custom-call | tf_op jit(solution)/shard_map/infini/pallas_call | solution.py:523
  64.5 1.9 %copy.7 = bf16[256,1024]{1,0:T(8,128)(2,1)} copy(bf16[256,1024]{1,0:T(8,128)(2,1)} %infini.1) | data formatting | bytes 1048576

commit v4 on v3

--- a/solution.py
+++ b/solution.py
@@ -230,27 +230,28 @@
         n = tin[slot, pl.ds(HD, 16), :].astype(F32)
         past[pl.ds(0, 8), HD:] += n[:8] + n[8:]
 
-    def to_quad(d):
+    def to_next():
         return pltpu.make_async_remote_copy(
-            src_ref=tmsg, dst_ref=tin.at[quad], send_sem=ts.at[d], recv_sem=tr.at[quad],
+            src_ref=tmsg, dst_ref=tin.at[0], send_sem=ts.at[0], recv_sem=tr.at[0],
+            device_id={"seq_0": z + 1}, device_id_type=MESH)
+
+    def to_far(d, slot):
+        return pltpu.make_async_remote_copy(
+            src_ref=tsum, dst_ref=tin.at[slot], send_sem=ts.at[d], recv_sem=tr.at[slot],
             device_id={"seq_0": z + d}, device_id_type=MESH)
 
-    def to_upper(d):
-        return pltpu.make_async_remote_copy(
-            src_ref=tsum, dst_ref=tin.at[4], send_sem=ts.at[3 + d], recv_sem=tr.at[4],
-            device_id={"seq_0": z + d}, device_id_type=MESH)
+    def put_sum():
+        put(tsum, past[:, :HD] + terms[:, :HD], past[pl.ds(0, 8), HD:] + jnp.transpose(terms[:, HD:])[:8])
 
     norm_rows = jnp.transpose(terms[:, HD:])[:8]
     put(tmsg, terms[:, :HD], norm_rows)
     past[...] = jnp.zeros_like(past)
-    for d in (1, 2, 3):
-        @pl.when(quad + d < 4)
-        def _():
-            to_quad(d).start()
-
-    @pl.loop(4, 6)
-    def _(i):
-        forward(nth(i))
+
+    @pl.when(lax.rem(z, 2) == 0)
+    def _():
+        to_next().start()
+
+    forward(nth(4))
 
     gate = 1.0 / (1.0 + jnp.exp(-jnp.full((8, HD), beta_ref[place], F32)))[0:1]
 
@@ -341,16 +342,31 @@
 
         @pl.when(i == 1)
         def _():
+            @pl.when(quad == 1)
+            def _():
+                add_in(0)
+                put_sum()
+                for d in (1, 2):
+                    to_far(d, 1).start()
+
+            forward(nth(5))
+
+            @pl.when(z != 3)
+            def _():
+                forward(nth(6))
+
+        @pl.when(i == 3)
+        def _():
             @pl.when(z == 3)
             def _():
-                for slot in range(3):
-                    add_in(slot)
-                put(tsum, past[:, :HD] + terms[:, :HD], past[pl.ds(0, 8), HD:] + jnp.transpose(terms[:, HD:])[:8])
+                add_in(0)
+                add_in(1)
+                put_sum()
                 for d in (1, 2, 3, 4):
-                    to_upper(d).start()
-
-            for k in (6, 7):
-                forward(nth(k))
+                    to_far(d, 2).start()
+                forward(nth(6))
+
+            forward(nth(7))
 
     def finish(j):
         local = acc[rows(j), :HD] / acc[rows(j), HD:]
@@ -384,15 +400,17 @@
     meet_previous(3)
     meet_previous(2)
 
-    @pl.when(z != 3)
-    def _():
-        @pl.loop(0, quad)
-        def _(slot):
-            add_in(slot)
-
-        @pl.when(z > 3)
-        def _():
-            add_in(4)
+    @pl.when(z == 7)
+    def _():
+        add_in(0)
+
+    @pl.when((quad == 2) | (z == 7))
+    def _():
+        add_in(1)
+
+    @pl.when(z > 3)
+    def _():
+        add_in(2)
 
     norm_cols = jnp.transpose(jnp.broadcast_to(past[0:1, HD:], (HD, HD)))
     full = jnp.concatenate([past[:, :HD], norm_cols], axis=1)
@@ -503,15 +521,19 @@
         def _():
             back(p).wait_send()
 
-    for d in (1, 2, 3):
-        @pl.when(quad + d < 4)
-        def _():
-            to_quad(d).wait_send()
+    @pl.when(lax.rem(z, 2) == 0)
+    def _():
+        to_next().wait_send()
+
+    @pl.when(quad == 1)
+    def _():
+        for d in (1, 2):
+            to_far(d, 1).wait_send()
 
     @pl.when(z == 3)
     def _():
         for d in (1, 2, 3, 4):
-            to_upper(d).wait_send()
+            to_far(d, 2).wait_send()
 
 
 def layer(queries, keys, values, beta, w_out):

time: 66.5 us -> 65.2 us (0.980)
  Pallas kernels: 64.5 us -> 62.9 us
    pallas_call x1, Pallas kernels: 64.5 us -> 62.9 us  [layer(): pl.pallas_call(body, name='infini', out_shape=jax.ShapeDtypeStruct((token...]
where the time goes in v4:
time: 65.2 us; the launch traced here: 64.8 us
  Pallas kernels  62.9 us (96%)
  local copies, waits for them, and re-layouts  1.87 us (3%)
    pallas_call x1, Pallas kernels, layer(): pl.pallas_call(body, name='infini', out_shape=jax.ShapeDtypeStruct((token...  62.9 us
    unnamed x1, local copies, waits for them, and re-layouts  1.87 us

profile of v4, /device:TPU:160, one launch (start us, length us, event | category | flops | bytes accessed | tf_op | source)
XLA Modules:
  0.0 64.8 jit_solution(687542850845255701)
XLA Ops:
  0.0 62.9 %infini.1 = bf16[256,1024]{1,0:T(8,128)(2,1)} custom-call(bf16[256,1024]{1,0:T(8,128)(2,1)} %q_hbm.1, bf16[256,1024]{1,0:T(8,128)(2,1)} %k_hbm.1, bf16[256,1024]{1,0:T(8,128)(2,1)} %v_hbm.1, f32[8]{0:T(128)} %beta_ref.1, bf16[1024,4096]{1,0:T(8,128)(2,1)} %w_hbm.1), custom_call_target="tpu_custom_call" | custom-call | tf_op jit(solution)/shard_map/infini/pallas_call | solution.py:545
  62.9 1.9 %copy.7 = bf16[256,1024]{1,0:T(8,128)(2,1)} copy(bf16[256,1024]{1,0:T(8,128)(2,1)} %infini.1) | data formatting | bytes 1048576

commit v5 on v4

--- a/solution.py
+++ b/solution.py
@@ -253,6 +253,10 @@
 
     forward(nth(4))
 
+    @pl.when(quad != 1)
+    def _():
+        forward(nth(5))
+
     gate = 1.0 / (1.0 + jnp.exp(-jnp.full((8, HD), beta_ref[place], F32)))[0:1]
 
     def back(j):
@@ -348,8 +352,7 @@
                 put_sum()
                 for d in (1, 2):
                     to_far(d, 1).start()
-
-            forward(nth(5))
+                forward(nth(5))
 
             @pl.when(z != 3)
             def _():

time: 65.2 us -> 65.2 us (level)
  no operation moved by 1% of the time
where the time goes in v5:
time: 65.2 us; the launch traced here: 64.8 us
  Pallas kernels  62.9 us (96%)
  local copies, waits for them, and re-layouts  1.87 us (3%)
    pallas_call x1, Pallas kernels, layer(): pl.pallas_call(body, name='infini', out_shape=jax.ShapeDtypeStruct((token...  62.9 us
    unnamed x1, local copies, waits for them, and re-layouts  1.87 us

profile of v5, /device:TPU:160, one launch (start us, length us, event | category | flops | bytes accessed | tf_op | source)
XLA Modules:
  0.0 64.8 jit_solution(18313504647504149074)
XLA Ops:
  0.0 62.9 %infini.1 = bf16[256,1024]{1,0:T(8,128)(2,1)} custom-call(bf16[256,1024]{1,0:T(8,128)(2,1)} %q_hbm.1, bf16[256,1024]{1,0:T(8,128)(2,1)} %k_hbm.1, bf16[256,1024]{1,0:T(8,128)(2,1)} %v_hbm.1, f32[8]{0:T(128)} %beta_ref.1, bf16[1024,4096]{1,0:T(8,128)(2,1)} %w_hbm.1), custom_call_target="tpu_custom_call" | custom-call | tf_op jit(solution)/shard_map/infini/pallas_call | solution.py:548
  62.9 1.9 %copy.7 = bf16[256,1024]{1,0:T(8,128)(2,1)} copy(bf16[256,1024]{1,0:T(8,128)(2,1)} %infini.1) | data formatting | bytes 1048576
